TPU v7x, 128 devices: a whole 4x4x4 slice. The times are simulated.
128 devices in a mesh: tok: 32 (over y_lo, z, x), voc: 4 (over y_hi, core).
Axes of the slice: x: 4, y: 4 (y_hi: 2, y_lo: 2; y = y_hi * 2 + y_lo), z: 4, core: 2. Of those that a mesh axis runs over, the one named last changes fastest.
Arguments:
- hidden: bfloat16 [1024, 3584], P('tok'), may hold values from -700 to 700
- teacher_logits: bfloat16 [1024, 81920], P(None, ('tok', 'voc')), may hold values from -300 to 300
- sampled_ids: int32 [1024], P('tok'), may hold values from 0 to 81919
- loss_mask: int32 [1024], P('tok'), may hold values from 0 to 1, as said below
- student_head: bfloat16 [3584, 81920], P(None, ('tok', 'voc')), may hold values from -0.3125 to 0.3125
Outputs:
- loss: float32 [], replicated
- sampled_ratio: float32 [1024], P(('tok', 'voc'))
- hidden_grad: bfloat16 [1024, 3584], P(('tok', 'voc'))
- head_grad: bfloat16 [3584, 81920], P(None, ('tok', 'voc'))
Inputs may be any that keep to these rules, and one draw needn't show every extreme that they name: `loss_mask`: at least one position is valid.
All inputs are finite; a program needn't handle non-finite values.
Results may differ from a plain program's by a relative error of at most 0.02.
Values may be sent and summed in bfloat16 or wider, within the bound.
No kernel may reach another device: no remote copies, remote signals or barrier semaphores. Data moves between devices by JAX's collectives and lax.ppermute only.
A program may use at most 128 MiB of HBM per device.

v0:
```python
import jax
import jax.numpy as jnp
from jax import lax
from jax.sharding import Mesh
from jax.sharding import PartitionSpec as P

TOK = ("tok_0", "tok_1", "tok_2")
TOK_VOC = ("tok_0", "tok_1", "tok_2", "voc_0", "voc_1")
VOC = ("voc_0", "voc_1")


def all_in_one(shard, axis):
    leaves = jax.tree.leaves(shard)
    order = sorted(range(len(leaves)), key=lambda k: -leaves[k].size)
    width = (1, *leaves[order[0]].shape)[-1]
    lines = [
        jnp.pad(leaves[k].reshape(-1), (0, -leaves[k].size % width)).reshape(-1, width)
        for k in order
    ]
    both, at, found = (lax.all_gather(jnp.concatenate(lines), axis), 0, {})
    for k, line in zip(order, lines):
        share = both[:, at : at + len(line)].reshape(len(both), -1)
        found[k] = share[:, : leaves[k].size].reshape(-1, *leaves[k].shape)
        at += len(line)
    numbers = iter(range(len(leaves)))
    return jax.tree.map(lambda _: found[next(numbers)], shard)


def combined_by_axis(shard, axes, combine):
    for axis in axes:
        pieces = all_in_one(shard, axis)
        shard = jax.tree.map(lambda part: part[0], pieces)
        for k in range(1, lax.axis_size(axis)):
            shard = combine(shard, jax.tree.map(lambda part: part[k], pieces))
    return shard


def sum_in_order(blocks, axes, order):
    inside = blocks.shape[1:]
    blocks = blocks.reshape(*(lax.axis_size(a) for a in axes), *inside)
    blocks = jnp.moveaxis(blocks, order, range(len(axes))).reshape(-1, *inside)
    for k in order:
        blocks = lax.psum_scatter(blocks, axes[k], scatter_dimension=0, tiled=True)
    return blocks[0]


def in_blocks(shard, dim, devices):
    before, after = (shard.shape[:dim], shard.shape[dim + 1 :])
    return jnp.moveaxis(shard.reshape(*before, devices, -1, *after), dim, 0)


def scatter_axes(shard, axes, order, dim):
    devices = lax.axis_size(axes)
    return sum_in_order(in_blocks(shard, dim, devices), axes, order)


def summed_on_arrival(shard, axis, dim):
    devices = lax.axis_size(axis)
    blocks = lax.all_to_all(in_blocks(shard, dim, devices), axis, 0, 0, tiled=True)
    return jnp.sum(blocks.astype(jnp.float32), axis=0)


def combine_stats(first, second):
    smax_a, stot_a, cross_a, tmax_a, ttot_a, spick_a, tpick_a = first
    smax_b, stot_b, cross_b, tmax_b, ttot_b, spick_b, tpick_b = second
    student_max = jnp.maximum(smax_a, smax_b)
    teacher_max = jnp.maximum(tmax_a, tmax_b)
    factor_a = jnp.exp(smax_a - student_max)
    factor_b = jnp.exp(smax_b - student_max)
    student_total = stot_a * factor_a + stot_b * factor_b
    cross_term = cross_a * factor_a + cross_b * factor_b
    teacher_total = ttot_a * jnp.exp(tmax_a - teacher_max) + ttot_b * jnp.exp(tmax_b - teacher_max)
    return (
        student_max,
        student_total,
        cross_term,
        teacher_max,
        teacher_total,
        spick_a + spick_b,
        tpick_a + tpick_b,
    )


def per_device(hidden, teacher_logits, sampled_ids, loss_mask, student_head):
    all_hidden, all_ids, all_mask = (
        lax.all_gather(hidden, TOK, axis=0, tiled=True),
        lax.all_gather(sampled_ids, TOK, axis=0, tiled=True),
        lax.all_gather(loss_mask, TOK, axis=0, tiled=True),
    )
    teacher = teacher_logits.astype(jnp.float32)
    student = jnp.dot(all_hidden, student_head, preferred_element_type=jnp.float32)
    devices = lax.axis_size(TOK_VOC)
    position = lax.axis_index(TOK_VOC)
    vocab_dev = student_head.shape[1]
    rows_all = all_hidden.shape[0]
    rows_own = rows_all // devices
    weight = all_mask.astype(jnp.float32)
    count = jnp.sum(weight)
    columns = position * vocab_dev + lax.broadcasted_iota(jnp.int32, (1, vocab_dev), 1)
    chosen = all_ids[:, None] == columns
    local_smax = jnp.max(student, axis=1)
    local_tmax = jnp.max(teacher, axis=1)
    shifted = jnp.exp(student - local_smax[:, None])
    local_stats = (
        local_smax,
        jnp.sum(shifted, axis=1),
        jnp.sum(shifted * (student - teacher), axis=1),
        local_tmax,
        jnp.sum(jnp.exp(teacher - local_tmax[:, None]), axis=1),
        jnp.sum(jnp.where(chosen, student, 0.0), axis=1),
        jnp.sum(jnp.where(chosen, teacher, 0.0), axis=1),
    )
    merged = combined_by_axis(local_stats, TOK_VOC, combine_stats)
    (
        student_max,
        student_total,
        cross_term,
        teacher_max,
        teacher_total,
        student_pick,
        teacher_pick,
    ) = merged
    student_shift = student_max + jnp.log(student_total)
    teacher_shift = teacher_max + jnp.log(teacher_total)
    row_kl = cross_term / student_total - student_shift + teacher_shift
    ratio_all = student_pick - student_shift - (teacher_pick - teacher_shift)
    sampled_ratio = lax.dynamic_slice_in_dim(ratio_all, position * rows_own, rows_own, 0)
    student_log = student - student_shift[:, None]
    differ = student_log - (teacher - teacher_shift[:, None])
    dlogits = (weight[:, None] * jnp.exp(student_log) * (differ - row_kl[:, None])).astype(
        jnp.bfloat16
    )
    loss = jnp.sum(weight * row_kl) / count
    partial_sum = scatter_axes(
        lax.dot_general(
            dlogits, student_head, (((1,), (1,)), ((), ())), preferred_element_type=jnp.float32
        ).astype(jnp.bfloat16),
        TOK,
        (1, 2, 0),
        0,
    ).astype(jnp.float32)
    hidden_sum = summed_on_arrival(partial_sum.astype(jnp.bfloat16), VOC, 0)
    hidden_grad = hidden_sum.astype(jnp.bfloat16)
    head_grad = lax.dot_general(
        all_hidden, dlogits, (((0,), (0,)), ((), ())), preferred_element_type=jnp.float32
    ).astype(jnp.bfloat16)
    return (loss, sampled_ratio, hidden_grad, head_grad)


def solution(mesh):
    split = Mesh(mesh.devices.reshape(2, 4, 4, 2, 2), ("tok_0", "tok_1", "tok_2", "voc_0", "voc_1"))
    in_specs = (P(TOK, None), P(None, TOK_VOC), P(TOK), P(TOK), P(None, TOK_VOC))
    out_specs = (P(), P(TOK_VOC), P(TOK_VOC, None), P(None, TOK_VOC))
    return jax.shard_map(
        per_device, mesh=split, in_specs=in_specs, out_specs=out_specs, check_vma=False
    )
```

profile of v0, /device:TPU:1, one launch (start us, length us, event | category | flops | bytes accessed | tf_op | source)
XLA Modules:
  0.0 395.3 jit_solution(10163011717840257338)
XLA Ops:
  7.2 0.0 copy-start.4
  7.2 0.0 all-gather.12.cloned.1.call-start
  7.3 0.7 all-gather.12.cloned.1.call-update
  7.9 0.0 reduce-scatter.4.cloned.1.call-start
  8.0 1.6 copy.14
  9.6 0.2 reduce_max.28
  9.9 0.0 copy-done.4
  9.9 0.6 dynamic-slice
  11.2 0.2 dynamic-update-slice
  11.4 0.2 dynamic-update-slice.1
  11.6 17.6 %all-reduce.2 = (s32[1024]{0:T(1024)S(1)}, s32[1024]{0:T(1024)S(1)}) all-reduce(s32[1024]{0:T(1024)S(1)} %dynamic-update-slice, s32[1024]{0:T(1024)S(1)} %dynamic-update-slice.1), channel_id=1, replica_groups=mesh['tok_0'=2,'tok_1'=4,'tok_2'=4,'voc_0'=2,'voc_1'=2] {'tok_0','tok_1'..., use_global_device_ids=true, to_apply=%add | all-reduce | flops 2048 | bytes 16384
  29.3 127.6 %all-gather.12.cloned.1.call-done = bf16[1024,3584]{1,0:T(8,128)(2,1)} async-done(((bf16[32,3584]{1,0:T(8,128)(2,1)}), bf16[1024,3584]{1,0:T(8,128)(2,1)}) %all-gather.12.cloned.1.call-update) | async-done | bytes 7340048 | tf_op jit(solution)/shard_map/all_gather | solution.py:86
  156.9 8.6 %fusion.119 = (f32[1024]{0:T(1024)S(1)}, f32[1024,640]{0,1:T(8,128)S(1)}) fusion(bf16[1024,3584]{1,0:T(8,128)(2,1)} %all-gather.12.cloned.1.call-done, bf16[3584,640]{1,0:T(8,128)(2,1)} %param.9), kind=kOutput, calls=%fused_computation.224 | convolution fusion | flops 4698274816 | bytes 14553088 | tf_op jit(solution)/shard_map/dot_general | solution.py:91
  165.5 0.0 copy-start
  165.6 1.5 copy-done
  167.0 1.8 fusion.3
  168.8 0.1 concatenate.15
  168.9 3.8 all-gather.5
  172.8 0.1 concatenate.16
  172.9 9.1 %all-gather.6 = f32[4,7,1024]{2,1,0:T(8,128)S(1)} all-gather(f32[1,7,1024]{2,1,0:T(8,128)S(1)} %bitcast.598), channel_id=3, replica_groups=mesh['tok_0'=2,'tok_1'=4,'tok_2'=4,'voc_0'=2,'voc_1'=2] {'tok_1'}, dimensions={0}, use_global_device_ids=true | all-gather | bytes 143360 | tf_op jit(solution)/shard_map/all_gather | solution.py:20
  182.0 0.1 fusion.55
  182.1 0.1 fusion.73
  182.2 0.1 concatenate.17
  182.2 9.1 %all-gather.7 = f32[4,7,1024]{2,1,0:T(8,128)S(1)} all-gather(f32[1,7,1024]{2,1,0:T(8,128)S(1)} %bitcast.599), channel_id=4, replica_groups=mesh['tok_0'=2,'tok_1'=4,'tok_2'=4,'voc_0'=2,'voc_1'=2] {'tok_2'}, dimensions={0}, use_global_device_ids=true | all-gather | bytes 143360 | tf_op jit(solution)/shard_map/all_gather | solution.py:20
  191.4 0.1 fusion.26
  191.5 0.1 fusion.44
  191.5 0.1 concatenate.18
  191.6 4.9 %all-gather.8 = f32[2,7,1024]{2,1,0:T(8,128)S(1)} all-gather(f32[1,7,1024]{2,1,0:T(8,128)S(1)} %bitcast.600), channel_id=5, replica_groups=mesh['tok_0'=2,'tok_1'=4,'tok_2'=4,'voc_0'=2,'voc_1'=2] {'voc_0'}, dimensions={0}, use_global_device_ids=true | all-gather | bytes 86016 | tf_op jit(solution)/shard_map/all_gather | solution.py:20
  196.6 0.1 concatenate.19
  196.7 30.3 %all-gather.9 = f32[2,7,1024]{2,1,0:T(8,128)S(1)} all-gather(f32[1,7,1024]{2,1,0:T(8,128)S(1)} %bitcast.601), channel_id=6, replica_groups=mesh['tok_0'=2,'tok_1'=4,'tok_2'=4,'voc_0'=2,'voc_1'=2] {'voc_1'}, dimensions={0}, use_global_device_ids=true | all-gather | bytes 86016 | tf_op jit(solution)/shard_map/all_gather | solution.py:20
  227.1 0.6 convert_reduce_fusion
  227.7 2.6 fusion.10
  230.2 8.5 %convolution_convert_fusion = bf16[1024,3584]{1,0:T(8,128)(2,1)S(1)} fusion(bf16[1024,640]{0,1:T(8,128)(2,1)S(1)} %fusion.10, bf16[3584,640]{1,0:T(8,128)(2,1)} %param.9), kind=kOutput, calls=%fused_computation | convolution fusion | flops 4701290496 | bytes 13238272 | tf_op jit(solution)/shard_map/dot_general | solution.py:135
  238.7 3.8 copy.15
  242.5 0.0 reduce-scatter.4.cloned.1.call-update
  242.6 0.0 reduce-scatter.6.cloned.1.call-start
  242.6 72.9 %reduce-scatter.4.cloned.1.call-done = bf16[8,32,3584]{2,1,0:T(8,128)(2,1)} async-done(((bf16[32,32,3584]{2,1,0:T(8,128)(2,1)}), bf16[8,32,3584]{2,1,0:T(8,128)(2,1)}) %reduce-scatter.4.cloned.1.call-update) | async-done | bytes 1835024 | tf_op jit(solution)/shard_map/reduce_scatter | solution.py:43
  315.5 0.0 reduce-scatter.6.cloned.1.call-update
  315.5 0.0 reduce-scatter.8.cloned.1.call-start
  315.6 29.5 %reduce-scatter.6.cloned.1.call-done = bf16[2,32,3584]{2,1,0:T(8,128)(2,1)} async-done(((bf16[8,32,3584]{2,1,0:T(8,128)(2,1)}), bf16[2,32,3584]{2,1,0:T(8,128)(2,1)}) %reduce-scatter.6.cloned.1.call-update) | async-done | bytes 458768 | tf_op jit(solution)/shard_map/reduce_scatter | solution.py:43
  345.1 0.0 reduce-scatter.8.cloned.1.call-update
  345.1 18.3 %reduce-scatter.8.cloned.1.call-done = bf16[1,32,3584]{2,1,0:T(8,128)(2,1)} async-done(((bf16[2,32,3584]{2,1,0:T(8,128)(2,1)}), bf16[1,32,3584]{2,1,0:T(8,128)(2,1)}) %reduce-scatter.8.cloned.1.call-update) | async-done | bytes 229392 | tf_op jit(solution)/shard_map/reduce_scatter | solution.py:43
  363.4 4.8 %all-to-all-start = ((bf16[4,8,3584]{2,1,0:T(8,128)(2,1)}), bf16[4,8,3584]{2,1,0:T(8,128)(2,1)S(1)}, u32[]{:S(2)}, u32[]{:S(2)}) async-start(bf16[4,8,3584]{2,1,0:T(8,128)(2,1)} %bitcast.596), calls=%async_computation.3 | async-start | bytes 458752 | tf_op jit(solution)/shard_map/all_to_all | solution.py:59
  368.2 9.6 %fusion = bf16[3584,640]{0,1:T(8,128)(2,1)} fusion(bf16[1024,640]{0,1:T(8,128)(2,1)S(1)} %fusion.10, bf16[1024,3584]{1,0:T(8,128)(2,1)} %all-gather.12.cloned.1.call-done), kind=kOutput, calls=%fused_computation.2 | convolution fusion | flops 4699914240 | bytes 13238272 | tf_op jit(solution)/shard_map/dot_general | solution.py:144
  377.8 7.2 %copy.16 = bf16[3584,640]{1,0:T(8,128)(2,1)} copy(bf16[3584,640]{0,1:T(8,128)(2,1)} %fusion) | data formatting | bytes 9175040
  386.4 0.6 dynamic_slice.3
  387.0 0.0 all-to-all-done
  387.0 0.7 reduce_sum.82
  (21 shorter events, 0.3 us)
Async XLA Ops:
  7.2 2.7 copy-start.4
  7.2 2.4 copy-start.1
  7.2 4.0 %copy-start.2 = (s32[32]{0:T(128)S(1)}, s32[32]{0:T(128)}, u32[]{:S(2)}) copy-start(s32[32]{0:T(128)} %param.8) | copy-start | bytes 388
  7.2 4.2 %copy-start.3 = (s32[32]{0:T(128)S(1)}, s32[32]{0:T(128)}, u32[]{:S(2)}) copy-start(s32[32]{0:T(128)} %param.7) | copy-start | bytes 388
  7.2 149.7 %all-gather.12.cloned.1.call-start = ((), (), s32[]{:S(2)}) async-start(), calls=%async_computation.4 | async-start | bytes 7569408 | tf_op jit(solution)/shard_map/all_gather | solution.py:86
  7.9 307.6 %reduce-scatter.4.cloned.1.call-start = ((), (), s32[]{:S(2)}) async-start(), calls=%async_computation.5 | async-start | bytes 9175040 | tf_op jit(solution)/shard_map/reduce_scatter | solution.py:43
  165.5 1.5 copy-start
  242.6 102.5 %reduce-scatter.6.cloned.1.call-start = ((), (), s32[]{:S(2)}) async-start(), calls=%async_computation.6 | async-start | bytes 2293760 | tf_op jit(solution)/shard_map/reduce_scatter | solution.py:43
  315.5 47.9 %reduce-scatter.8.cloned.1.call-start = ((), (), s32[]{:S(2)}) async-start(), calls=%async_computation.7 | async-start | bytes 688128 | tf_op jit(solution)/shard_map/reduce_scatter | solution.py:43
  363.4 23.6 %all-to-all-start = ((bf16[4,8,3584]{2,1,0:T(8,128)(2,1)}), bf16[4,8,3584]{2,1,0:T(8,128)(2,1)S(1)}, u32[]{:S(2)}, u32[]{:S(2)}) async-start(bf16[4,8,3584]{2,1,0:T(8,128)(2,1)} %bitcast.596), calls=%async_computation.3 | async-start | bytes 458752 | tf_op jit(solution)/shard_map/all_to_all | solution.py:59
Sparse Core Ops, SparseCore 0:
  9.7 147.2 all-gather.11
  242.7 72.7 reduce-scatter.3
  317.9 27.0 reduce-scatter.5
  347.3 16.0 reduce-scatter.7
where the time goes:
time: 396 us; the launch traced here: 395 us
  waiting for transfers between devices  249 us (63%)
  blocking collectives  74.9 us (19%)
  matrix products  26.7 us (7%)
  between operations  17.1 us (4%)
  local copies, waits for them, and re-layouts  16.1 us (4%)
  other arithmetic  6.47 us (2%)
  starting transfers between devices  4.97 us (1%)
    all_gather x1, waiting for transfers between devices, per_device(): lax.all_gather(hidden, TOK, axis=0, tiled=True)  128 us
    reduce_scatter x3, waiting for transfers between devices, sum_in_order(): blocks = lax.psum_scatter(blocks, axes[k], scatter_dimension=0, tiled=True)  121 us
    all_gather x5, blocking collectives, all_in_one(): both, at, found = (lax.all_gather(jnp.concatenate(lines), axis), 0, {})  57.3 us
    unnamed x1, blocking collectives  17.6 us
    unnamed x17, local copies, waits for them, and re-layouts  11.4 us
    dot_general x1, matrix products, per_device(): lax.dot_general(all_hidden, dlogits, (((0,), (0,)), ((), ())), preferred_...  9.57 us
    dot_general x1, matrix products, per_device(): jnp.dot(all_hidden, student_head, preferred_element_type=jnp.float32)  8.63 us
    dot_general x1, matrix products, per_device(): lax.dot_general(dlogits, student_head, (((1,), (1,)), ((), ())), preferre...  8.51 us
  transfers between devices with their start and end apart: 5, of which 4 were waited for; matrix products, arithmetic and copies ran while one was open for 5% of the time, Pallas kernels for 0%

commit v1 on v0

--- a/solution.py
+++ b/solution.py
@@ -83,7 +83,9 @@
 
 def per_device(hidden, teacher_logits, sampled_ids, loss_mask, student_head):
     all_hidden, all_ids, all_mask = (
-        lax.all_gather(hidden, TOK, axis=0, tiled=True),
+        jnp.concatenate(
+            lax.all_to_all(jnp.stack([hidden] * lax.axis_size(TOK)), TOK, 0, 0), axis=0
+        ),
         lax.all_gather(sampled_ids, TOK, axis=0, tiled=True),
         lax.all_gather(loss_mask, TOK, axis=0, tiled=True),
     )

time: 396 us -> 356 us (0.90)
  waiting for transfers between devices: 249 us -> 118 us
  blocking collectives: 74.9 us -> 151 us
  starting transfers between devices: 4.97 us -> 14.9 us
    all_gather x1 -> x0, waiting for transfers between devices: 128 us -> none  [per_device(): lax.all_gather(hidden, TOK, axis=0, tiled=True)]
    unnamed x1, blocking collectives: 17.6 us -> 108 us
    all_gather x5, blocking collectives: 57.3 us -> 43 us  [all_in_one(): both, at, found = (lax.all_gather(jnp.concatenate(lines), axis), 0, {})]
    all_to_all x0 -> x1, starting transfers between devices: none -> 9.96 us  [per_device(): lax.all_to_all(jnp.stack([hidden] * lax.axis_size(TOK)), TOK, 0, 0)]
    another operation x0 -> x1, local copies, waits for them, and re-layouts: none -> 4.79 us  [per_device(): jnp.stack([hidden] * lax.axis_size(TOK))]
  transfers between devices with their start and end apart: 5 -> 5, of which waited for: 4 -> 3; matrix products, arithmetic and copies ran while one was open for 5% -> 5% of each run, Pallas kernels for 0% -> 0%
where the time goes in v1:
time: 356 us; the launch traced here: 355 us
  blocking collectives  151 us (42%)
  waiting for transfers between devices  118 us (33%)
  matrix products  26.7 us (8%)
  local copies, waits for them, and re-layouts  19.9 us (6%)
  between operations  17.1 us (5%)
  starting transfers between devices  14.9 us (4%)
  other arithmetic  6.46 us (2%)
    reduce_scatter x3, waiting for transfers between devices, sum_in_order(): blocks = lax.psum_scatter(blocks, axes[k], scatter_dimension=0, tiled=True)  118 us
    unnamed x1, blocking collectives  108 us
    all_gather x5, blocking collectives, all_in_one(): both, at, found = (lax.all_gather(jnp.concatenate(lines), axis), 0, {})  43 us
    unnamed x17, local copies, waits for them, and re-layouts  10.5 us
    all_to_all x1, starting transfers between devices, per_device(): lax.all_to_all(jnp.stack([hidden] * lax.axis_size(TOK)), TOK, 0, 0)  9.96 us
    dot_general x1, matrix products, per_device(): lax.dot_general(all_hidden, dlogits, (((0,), (0,)), ((), ())), preferred_...  9.54 us
    dot_general x1, matrix products, per_device(): jnp.dot(all_hidden, student_head, preferred_element_type=jnp.float32)  8.64 us
    dot_general x1, matrix products, per_device(): lax.dot_general(dlogits, student_head, (((1,), (1,)), ((), ())), preferre...  8.5 us
  transfers between devices with their start and end apart: 5, of which 3 were waited for; matrix products, arithmetic and copies ran while one was open for 5% of the time, Pallas kernels for 0%

profile of v1, /device:TPU:1, one launch (start us, length us, event | category | flops | bytes accessed | tf_op | source)
XLA Modules:
  0.0 355.0 jit_solution(16312167515455385034)
XLA Ops:
  7.2 4.8 %stack.2 = bf16[32,32,3584]{2,1,0:T(8,128)(2,1)} broadcast(bf16[32,3584]{1,0:T(8,128)(2,1)} %param.5), dimensions={1,2} | broadcast | bytes 7569408 | tf_op jit(solution)/shard_map/stack | solution.py:87
  12.0 10.0 %all-to-all-start = ((bf16[32,32,3584]{2,1,0:T(8,128)(2,1)}), bf16[32,32,3584]{2,1,0:T(8,128)(2,1)}, u32[]{:S(2)}, u32[]{:S(2)}) async-start(bf16[32,32,3584]{2,1,0:T(8,128)(2,1)} %stack.2), calls=%async_computation | async-start | bytes 14680064 | tf_op jit(solution)/shard_map/all_to_all | solution.py:87
  21.9 0.0 copy-start.4
  21.9 0.0 copy-start.2
  21.9 0.0 copy-start.3
  22.0 0.0 reduce-scatter.4.cloned.1.call-start
  22.0 0.7 copy.14
  22.7 0.2 reduce_max.28
  23.0 0.6 dynamic-slice
  24.2 0.2 dynamic-update-slice
  24.5 0.2 dynamic-update-slice.1
  24.7 108.4 %all-reduce.2 = (s32[1024]{0:T(1024)S(1)}, s32[1024]{0:T(1024)S(1)}) all-reduce(s32[1024]{0:T(1024)S(1)} %dynamic-update-slice, s32[1024]{0:T(1024)S(1)} %dynamic-update-slice.1), channel_id=1, replica_groups=mesh['tok_0'=2,'tok_1'=4,'tok_2'=4,'voc_0'=2,'voc_1'=2] {'tok_0','tok_1'..., use_global_device_ids=true, to_apply=%add | all-reduce | flops 2048 | bytes 16384
  133.2 8.6 %fusion.119 = (f32[1024]{0:T(1024)S(1)}, f32[1024,640]{0,1:T(8,128)S(1)}) fusion(bf16[1024,3584]{1,0:T(8,128)(2,1)} %bitcast.1, bf16[3584,640]{1,0:T(8,128)(2,1)} %param.9), kind=kOutput, calls=%fused_computation.224 | convolution fusion | flops 4698274816 | bytes 14553088 | tf_op jit(solution)/shard_map/dot_general | solution.py:93
  141.8 0.0 copy-start
  141.8 1.5 copy-done
  143.3 1.8 fusion.3
  145.1 0.1 concatenate.15
  145.2 3.4 all-gather.5
  148.7 0.1 concatenate.16
  148.8 10.7 %all-gather.6 = f32[4,7,1024]{2,1,0:T(8,128)S(1)} all-gather(f32[1,7,1024]{2,1,0:T(8,128)S(1)} %bitcast.599), channel_id=3, replica_groups=mesh['tok_0'=2,'tok_1'=4,'tok_2'=4,'voc_0'=2,'voc_1'=2] {'tok_1'}, dimensions={0}, use_global_device_ids=true | all-gather | bytes 143360 | tf_op jit(solution)/shard_map/all_gather | solution.py:20
  159.5 0.1 fusion.55
  159.6 0.1 fusion.73
  159.7 0.1 concatenate.17
  159.7 9.2 %all-gather.7 = f32[4,7,1024]{2,1,0:T(8,128)S(1)} all-gather(f32[1,7,1024]{2,1,0:T(8,128)S(1)} %bitcast.600), channel_id=4, replica_groups=mesh['tok_0'=2,'tok_1'=4,'tok_2'=4,'voc_0'=2,'voc_1'=2] {'tok_2'}, dimensions={0}, use_global_device_ids=true | all-gather | bytes 143360 | tf_op jit(solution)/shard_map/all_gather | solution.py:20
  169.0 0.1 fusion.26
  169.1 0.1 fusion.44
  169.1 0.1 concatenate.18
  169.2 4.9 %all-gather.8 = f32[2,7,1024]{2,1,0:T(8,128)S(1)} all-gather(f32[1,7,1024]{2,1,0:T(8,128)S(1)} %bitcast.601), channel_id=5, replica_groups=mesh['tok_0'=2,'tok_1'=4,'tok_2'=4,'voc_0'=2,'voc_1'=2] {'voc_0'}, dimensions={0}, use_global_device_ids=true | all-gather | bytes 86016 | tf_op jit(solution)/shard_map/all_gather | solution.py:20
  174.2 0.1 concatenate.19
  174.3 14.8 %all-gather.9 = f32[2,7,1024]{2,1,0:T(8,128)S(1)} all-gather(f32[1,7,1024]{2,1,0:T(8,128)S(1)} %bitcast.602), channel_id=6, replica_groups=mesh['tok_0'=2,'tok_1'=4,'tok_2'=4,'voc_0'=2,'voc_1'=2] {'voc_1'}, dimensions={0}, use_global_device_ids=true | all-gather | bytes 86016 | tf_op jit(solution)/shard_map/all_gather | solution.py:20
  189.1 0.6 convert_reduce_fusion
  189.7 2.6 fusion.10
  192.3 8.5 %convolution_convert_fusion = bf16[1024,3584]{1,0:T(8,128)(2,1)S(1)} fusion(bf16[1024,640]{0,1:T(8,128)(2,1)S(1)} %fusion.10, bf16[3584,640]{1,0:T(8,128)(2,1)} %param.9), kind=kOutput, calls=%fused_computation | convolution fusion | flops 4701290496 | bytes 13238272 | tf_op jit(solution)/shard_map/dot_general | solution.py:137
  200.8 3.8 %copy.15 = bf16[2,4,4,32,3584]{4,3,0,2,1:T(8,128)(2,1)} copy(bf16[2,4,4,32,3584]{4,3,2,1,0:T(8,128)(2,1)S(1)} %bitcast.596) | data formatting | bytes 14680064 | tf_op jit(solution)/shard_map/reshape;reshape | solution.py:40
  204.6 0.0 reduce-scatter.4.cloned.1.call-update
  204.6 0.0 reduce-scatter.6.cloned.1.call-start
  204.7 70.4 %reduce-scatter.4.cloned.1.call-done = bf16[8,32,3584]{2,1,0:T(8,128)(2,1)} async-done(((bf16[32,32,3584]{2,1,0:T(8,128)(2,1)}), bf16[8,32,3584]{2,1,0:T(8,128)(2,1)}) %reduce-scatter.4.cloned.1.call-update) | async-done | bytes 1835024 | tf_op jit(solution)/shard_map/reduce_scatter | solution.py:43
  275.1 0.0 reduce-scatter.6.cloned.1.call-update
  275.1 0.0 reduce-scatter.8.cloned.1.call-start
  275.2 29.5 %reduce-scatter.6.cloned.1.call-done = bf16[2,32,3584]{2,1,0:T(8,128)(2,1)} async-done(((bf16[8,32,3584]{2,1,0:T(8,128)(2,1)}), bf16[2,32,3584]{2,1,0:T(8,128)(2,1)}) %reduce-scatter.6.cloned.1.call-update) | async-done | bytes 458768 | tf_op jit(solution)/shard_map/reduce_scatter | solution.py:43
  304.6 0.0 reduce-scatter.8.cloned.1.call-update
  304.7 18.5 %reduce-scatter.8.cloned.1.call-done = bf16[1,32,3584]{2,1,0:T(8,128)(2,1)} async-done(((bf16[2,32,3584]{2,1,0:T(8,128)(2,1)}), bf16[1,32,3584]{2,1,0:T(8,128)(2,1)}) %reduce-scatter.8.cloned.1.call-update) | async-done | bytes 229392 | tf_op jit(solution)/shard_map/reduce_scatter | solution.py:43
  323.1 4.8 %all-to-all-start.1 = ((bf16[4,8,3584]{2,1,0:T(8,128)(2,1)}), bf16[4,8,3584]{2,1,0:T(8,128)(2,1)S(1)}, u32[]{:S(2)}, u32[]{:S(2)}) async-start(bf16[4,8,3584]{2,1,0:T(8,128)(2,1)} %bitcast.597), calls=%async_computation.4 | async-start | bytes 458752 | tf_op jit(solution)/shard_map/all_to_all | solution.py:59
  328.0 9.5 %fusion = bf16[3584,640]{0,1:T(8,128)(2,1)} fusion(bf16[1024,640]{0,1:T(8,128)(2,1)S(1)} %fusion.10, bf16[1024,3584]{1,0:T(8,128)(2,1)} %bitcast.1), kind=kOutput, calls=%fused_computation.2 | convolution fusion | flops 4699914240 | bytes 13238272 | tf_op jit(solution)/shard_map/dot_general | solution.py:146
  337.5 7.2 %copy.16 = bf16[3584,640]{1,0:T(8,128)(2,1)} copy(bf16[3584,640]{0,1:T(8,128)(2,1)} %fusion) | data formatting | bytes 9175040
  346.1 0.6 dynamic_slice.3
  346.7 0.0 all-to-all-done.1
  346.7 0.7 reduce_sum.82
  (21 shorter events, 0.3 us)
Async XLA Ops:
  12.0 10.1 %copy-start.1 = (bf16[1024,640]{1,0:T(8,128)(2,1)S(1)}, bf16[1024,640]{1,0:T(8,128)(2,1)}, u32[]{:S(2)}) copy-start(bf16[1024,640]{1,0:T(8,128)(2,1)} %param.6) | copy-start | bytes 3932164
  12.0 121.2 %all-to-all-start = ((bf16[32,32,3584]{2,1,0:T(8,128)(2,1)}), bf16[32,32,3584]{2,1,0:T(8,128)(2,1)}, u32[]{:S(2)}, u32[]{:S(2)}) async-start(bf16[32,32,3584]{2,1,0:T(8,128)(2,1)} %stack.2), calls=%async_computation | async-start | bytes 14680064 | tf_op jit(solution)/shard_map/all_to_all | solution.py:87
  21.9 1.0 copy-start.4
  21.9 2.3 copy-start.2
  21.9 2.5 copy-start.3
  22.0 253.1 %reduce-scatter.4.cloned.1.call-start = ((), (), s32[]{:S(2)}) async-start(), calls=%async_computation.5 | async-start | bytes 9175040 | tf_op jit(solution)/shard_map/reduce_scatter | solution.py:43
  141.8 1.5 copy-start
  204.6 100.0 %reduce-scatter.6.cloned.1.call-start = ((), (), s32[]{:S(2)}) async-start(), calls=%async_computation.6 | async-start | bytes 2293760 | tf_op jit(solution)/shard_map/reduce_scatter | solution.py:43
  275.1 48.0 %reduce-scatter.8.cloned.1.call-start = ((), (), s32[]{:S(2)}) async-start(), calls=%async_computation.7 | async-start | bytes 688128 | tf_op jit(solution)/shard_map/reduce_scatter | solution.py:43
  323.1 23.5 %all-to-all-start.1 = ((bf16[4,8,3584]{2,1,0:T(8,128)(2,1)}), bf16[4,8,3584]{2,1,0:T(8,128)(2,1)S(1)}, u32[]{:S(2)}, u32[]{:S(2)}) async-start(bf16[4,8,3584]{2,1,0:T(8,128)(2,1)} %bitcast.597), calls=%async_computation.4 | async-start | bytes 458752 | tf_op jit(solution)/shard_map/all_to_all | solution.py:59
Sparse Core Ops, SparseCore 0:
  204.7 70.3 reduce-scatter.3
  277.5 27.0 reduce-scatter.5
  307.0 16.0 reduce-scatter.7
